TPU v7x, 32 devices: a whole 2x2x4 slice. The times are simulated.
32 devices in a mesh: dp: 8 (over z, y), tensor: 4 (over x, core).
Axes of the slice: x: 2, y: 2, z: 4, core: 2. Of those that a mesh axis runs over, the one named last changes fastest.
Arguments:
- tokens: bfloat16 [37632, 768], P(('dp', 'tensor')), may hold values from -21 to 21
- res_class: int32 [192], P('dp'), may hold values from 0 to 1
- gain_attn: float32 [768], replicated, may hold values from 0.5 to 1.5
- shift_attn: float32 [768], replicated, may hold values from -1.5 to 1.5
- w_qkv: bfloat16 [768, 3, 768], P(None, None, 'tensor'), may hold values from -0.3125 to 0.3125
- bias_qv: float32 [2, 768], P(None, 'tensor'), may hold values from -1.5 to 1.5
- w_out: bfloat16 [768, 768], P('tensor'), may hold values from -0.625 to 0.625
- bias_out: float32 [768], replicated, may hold values from -1.5 to 1.5
- gain_mlp: float32 [768], replicated, may hold values from 0.5 to 1.5
- shift_mlp: float32 [768], replicated, may hold values from -1.5 to 1.5
- w_up: bfloat16 [768, 3072], P(None, 'tensor'), may hold values from -0.21875 to 0.21875
- bias_up: float32 [3072], P('tensor'), may hold values from -1.5 to 1.5
- w_down: bfloat16 [3072, 768], P('tensor'), may hold values from -0.15625 to 0.15625
- bias_down: float32 [768], replicated, may hold values from -1.5 to 1.5
- cotangent: bfloat16 [37632, 768], P(('dp', 'tensor')), may hold values from -21 to 21
Outputs:
- block_out: bfloat16 [37632, 768], P(('dp', 'tensor'))
- grad_tokens: float32 [37632, 768], P(('dp', 'tensor'))
- grad_gain_attn: float32 [768], replicated
- grad_shift_attn: float32 [768], replicated
- grad_qkv: float32 [768, 3, 768], P(None, None, 'tensor')
- grad_bias_qv: float32 [2, 768], P(None, 'tensor')
- grad_out: float32 [768, 768], P('tensor')
- grad_bias_out: float32 [768], replicated
- grad_gain_mlp: float32 [768], replicated
- grad_shift_mlp: float32 [768], replicated
- grad_up: float32 [768, 3072], P(None, 'tensor')
- grad_bias_up: float32 [3072], P('tensor')
- grad_down: float32 [3072, 768], P('tensor')
- grad_bias_down: float32 [768], replicated
- rms: float32 [3], replicated
All inputs are finite; a program needn't handle non-finite values.
Results may differ from a plain program's by a relative error of at most 0.017.
Values may be sent and summed in bfloat16 or wider, within the bound.
A program may use at most 256 MiB of HBM per device.

v0:
```python
import jax
import jax.numpy as jnp
from jax import lax
from jax.sharding import PartitionSpec as P

HEAD_DIM = 64
PATCHES = 196
PATCHES_LOW = 144
EPS = 1e-06


def normalize(values):
    mean = jnp.mean(values, axis=-1, keepdims=True)
    centred = values - mean
    factor = lax.rsqrt(jnp.mean(centred * centred, axis=-1, keepdims=True) + EPS)
    return (centred * factor, factor)


def norm_back(grad_out, gain, normed, factor):
    scaled = grad_out * gain
    return factor * (
        scaled
        - jnp.mean(scaled, axis=-1, keepdims=True)
        - normed * jnp.mean(scaled * normed, axis=-1, keepdims=True)
    )


def exact_gelu(values):
    return jax.nn.gelu(values, approximate=False)


def on_device(
    tokens,
    res_class,
    gain_attn,
    shift_attn,
    w_qkv,
    bias_qv,
    w_out,
    bias_out,
    gain_mlp,
    shift_mlp,
    w_up,
    bias_up,
    w_down,
    bias_down,
    cotangent,
):
    rows = tokens.shape[0]
    width = tokens.shape[1]
    images = res_class.shape[0]
    local = w_qkv.shape[2]
    heads_here = local // HEAD_DIM
    scale = HEAD_DIM ** (-0.5)
    place = lax.axis_index("tensor")
    counts = jnp.where(res_class == 0, PATCHES, PATCHES_LOW)
    key_valid = jnp.arange(PATCHES)[None, :] < counts[:, None]
    flat_valid = key_valid.reshape(-1).astype(jnp.float32)
    row_valid = lax.dynamic_slice_in_dim(flat_valid, place * rows, rows)[:, None]
    mask = key_valid[:, None, None, :]
    shape = (images, PATCHES, heads_here, HEAD_DIM)
    w_qkv_flat = w_qkv.reshape(width, 3 * local)
    inputs = tokens.astype(jnp.float32)
    normed_a, factor_a = normalize(inputs)
    in_attn = (normed_a * gain_attn + shift_attn).astype(jnp.bfloat16)
    full_attn = lax.all_gather(in_attn, "tensor", axis=0, tiled=True)
    qkv = jnp.dot(full_attn, w_qkv_flat, preferred_element_type=jnp.float32).reshape(-1, 3, local)
    query = (qkv[:, 0] + bias_qv[0]).astype(jnp.bfloat16).reshape(shape)
    keys = qkv[:, 1].astype(jnp.bfloat16).reshape(shape)
    values = (qkv[:, 2] + bias_qv[1]).astype(jnp.bfloat16).reshape(shape)
    scores = jnp.einsum("iqhd,ikhd->ihqk", query, keys, preferred_element_type=jnp.float32) * scale
    scores = jnp.where(mask, scores, -1e30)
    log_total = jax.nn.logsumexp(scores, axis=-1, keepdims=True)
    probs = jnp.exp(scores - log_total).astype(jnp.bfloat16)
    context = (
        jnp.einsum("ihqk,ikhd->iqhd", probs, values, preferred_element_type=jnp.float32)
        .reshape(-1, local)
        .astype(jnp.bfloat16)
    )
    piece = context
    branch = (
        lax.psum_scatter(
            jnp.dot(piece, w_out, preferred_element_type=jnp.float32).astype(jnp.bfloat16),
            "tensor",
            scatter_dimension=0,
            tiled=True,
        ).astype(jnp.float32)
        + bias_out
    )
    hidden = inputs + branch
    normed_m, factor_m = normalize(hidden)
    in_mlp = (normed_m * gain_mlp + shift_mlp).astype(jnp.bfloat16)
    full_mlp = lax.all_gather(in_mlp, "tensor", axis=0, tiled=True)
    pre_act = jnp.dot(full_mlp, w_up, preferred_element_type=jnp.float32) + bias_up
    act = exact_gelu(pre_act).astype(jnp.bfloat16)
    piece = act
    mlp = (
        lax.psum_scatter(
            jnp.dot(piece, w_down, preferred_element_type=jnp.float32).astype(jnp.bfloat16),
            "tensor",
            scatter_dimension=0,
            tiled=True,
        ).astype(jnp.float32)
        + bias_down
    )
    stream = (hidden + mlp) * row_valid
    block_out = stream.astype(jnp.bfloat16)
    grad_stream = cotangent.astype(jnp.float32) * row_valid
    grad_bias_down = jnp.sum(grad_stream, axis=0)
    grad_mlp_full = lax.all_gather(grad_stream.astype(jnp.bfloat16), "tensor", axis=0, tiled=True)
    weight_down = jnp.einsum("tf,td->fd", act, grad_mlp_full, preferred_element_type=jnp.float32)
    grad_act = jnp.einsum("td,fd->tf", grad_mlp_full, w_down, preferred_element_type=jnp.float32)
    gelu_out, gelu_back = jax.vjp(exact_gelu, pre_act)
    grad_pre = gelu_back(grad_act)[0]
    grad_bias_up = jnp.sum(grad_pre, axis=0)
    grad_pre_low = grad_pre.astype(jnp.bfloat16)
    weight_up = jnp.einsum("td,tf->df", full_mlp, grad_pre_low, preferred_element_type=jnp.float32)
    piece = grad_pre_low
    grad_in_mlp = lax.psum_scatter(
        jnp.einsum("tf,df->td", piece, w_up, preferred_element_type=jnp.float32).astype(
            jnp.bfloat16
        ),
        "tensor",
        scatter_dimension=0,
        tiled=True,
    ).astype(jnp.float32)
    grad_gain_mlp = jnp.sum(grad_in_mlp * normed_m, axis=0)
    grad_shift_mlp = jnp.sum(grad_in_mlp, axis=0)
    grad_hidden = grad_stream + norm_back(grad_in_mlp, gain_mlp, normed_m, factor_m)
    grad_bias_out = jnp.sum(grad_hidden, axis=0)
    grad_branch_full = lax.all_gather(
        grad_hidden.astype(jnp.bfloat16), "tensor", axis=0, tiled=True
    )
    weight_out = jnp.einsum(
        "tc,td->cd", context, grad_branch_full, preferred_element_type=jnp.float32
    )
    grad_context = (
        jnp.einsum("td,cd->tc", grad_branch_full, w_out, preferred_element_type=jnp.float32)
        .astype(jnp.bfloat16)
        .reshape(shape)
    )
    again = jnp.einsum("iqhd,ikhd->ihqk", query, keys, preferred_element_type=jnp.float32) * scale
    again = jnp.where(mask, again, -1e30)
    probs_full = jnp.exp(again - log_total)
    probs_low = probs_full.astype(jnp.bfloat16)
    grad_value = jnp.einsum(
        "ihqk,iqhd->ikhd", probs_low, grad_context, preferred_element_type=jnp.float32
    )
    grad_probs = jnp.einsum(
        "iqhd,ikhd->ihqk", grad_context, values, preferred_element_type=jnp.float32
    )
    row_dot = jnp.sum(probs_full * grad_probs, axis=-1, keepdims=True)
    grad_scores = (probs_full * (grad_probs - row_dot)).astype(jnp.bfloat16)
    grad_query = scale * jnp.einsum(
        "ihqk,ikhd->iqhd", grad_scores, keys, preferred_element_type=jnp.float32
    )
    grad_key = scale * jnp.einsum(
        "ihqk,iqhd->ikhd", grad_scores, query, preferred_element_type=jnp.float32
    )
    query_low = grad_query.reshape(-1, local).astype(jnp.bfloat16)
    key_low = grad_key.reshape(-1, local).astype(jnp.bfloat16)
    value_low = grad_value.reshape(-1, local).astype(jnp.bfloat16)
    grad_bias_qv = jnp.stack(
        [
            jnp.sum(query_low.astype(jnp.float32), axis=0),
            jnp.sum(value_low.astype(jnp.float32), axis=0),
        ]
    )
    grad_qkv_low = jnp.stack([query_low, key_low, value_low], axis=1).reshape(-1, 3 * local)
    weight_qkv = jnp.einsum(
        "td,tc->dc", full_attn, grad_qkv_low, preferred_element_type=jnp.float32
    ).reshape(width, 3, local)
    piece = grad_qkv_low
    grad_in_attn = lax.psum_scatter(
        jnp.einsum("tc,dc->td", piece, w_qkv_flat, preferred_element_type=jnp.float32).astype(
            jnp.bfloat16
        ),
        "tensor",
        scatter_dimension=0,
        tiled=True,
    ).astype(jnp.float32)
    grad_gain_attn = jnp.sum(grad_in_attn * normed_a, axis=0)
    grad_shift_attn = jnp.sum(grad_in_attn, axis=0)
    grad_tokens = grad_hidden + norm_back(grad_in_attn, gain_attn, normed_a, factor_a)
    totals = jnp.stack(
        [
            jnp.sum(stream * stream),
            jnp.sum(branch * branch * row_valid),
            jnp.sum(mlp * mlp * row_valid),
            jnp.sum(row_valid),
        ]
    )
    summed = lax.psum(
        (
            grad_gain_attn,
            grad_shift_attn,
            grad_bias_out,
            grad_gain_mlp,
            grad_shift_mlp,
            grad_bias_down,
            totals,
        ),
        ("dp", "tensor"),
    )
    weight_qkv, grad_bias_qv, weight_out, weight_up, grad_bias_up, weight_down = lax.psum(
        (weight_qkv, grad_bias_qv, weight_out, weight_up, grad_bias_up, weight_down), "dp"
    )
    sums = summed[6]
    rms = jnp.sqrt(sums[:3] / (sums[3] * width))
    return (
        block_out,
        grad_tokens,
        summed[0],
        summed[1],
        weight_qkv,
        grad_bias_qv,
        weight_out,
        summed[2],
        summed[3],
        summed[4],
        weight_up,
        grad_bias_up,
        weight_down,
        summed[5],
        rms,
    )


def solution(mesh):
    in_specs = (
        P(("dp", "tensor"), None),
        P("dp"),
        P(),
        P(),
        P(None, None, "tensor"),
        P(None, "tensor"),
        P("tensor", None),
        P(),
        P(),
        P(),
        P(None, "tensor"),
        P("tensor"),
        P("tensor", None),
        P(),
        P(("dp", "tensor"), None),
    )
    out_specs = (
        P(("dp", "tensor"), None),
        P(("dp", "tensor"), None),
        P(),
        P(),
        P(None, None, "tensor"),
        P(None, "tensor"),
        P("tensor", None),
        P(),
        P(),
        P(),
        P(None, "tensor"),
        P("tensor"),
        P("tensor", None),
        P(),
        P(),
    )
    return jax.shard_map(
        on_device, mesh=mesh, in_specs=in_specs, out_specs=out_specs, check_vma=False
    )
```

profile of v0, /device:TPU:0, one launch (start us, length us, event | category | flops | bytes accessed | tf_op | source)
XLA Modules:
  0.0 985.3 jit_solution(16900257428672392909)
XLA Ops:
  7.3 2.0 convert_reduce_fusion.2
  9.2 2.1 fusion.30
  12.0 2.6 fusion.26
  16.8 52.4 %all-gather.5.cloned.1.call-done = bf16[4704,768]{1,0:T(8,128)(2,1)} async-done(((bf16[1176,768]{1,0:T(8,128)(2,1)}), bf16[4704,768]{1,0:T(8,128)(2,1)}) %all-gather.5.cloned.1.call-update) | async-done | bytes 7225360 | tf_op jit(solution)/shard_map/all_gather | solution.py:66
  69.2 7.3 fusion.10
  76.5 1.4 slice.36
  77.9 3.4 fusion.73
  81.4 6.0 convert_element_type.155
  87.4 6.4 squeeze.9
  93.9 6.4 squeeze.8
  100.3 7.4 fusion.6
  108.3 4.7 exponential_reduce_fusion
  114.0 11.1 %convert_bitcast_fusion = bf16[24,196,3,64]{1,3,2,0:T(8,128)(2,1)S(1)} fusion(f32[24,196,3,64]{1,0,3,2:T(8,128)} %squeeze.8, f32[3,64]{1,0:T(4,128)} %add.138, f32[24,3,196,196]{2,3,1,0:T(8,128)} %copy-done.2, f32[24,3,196]{2,1,0:T(4,128)S(1)} %log_add_fusion, pred[24,196]{1,0:T(8,128)(4,1)S(1)} %get-tuple-element.54), kind=kOutput, calls=%fused_computation.91 | convolution fusion | flops 367815168 | bytes 16544736 | tf_op jit(solution)/shard_map/ihqk,ikhd->iqhd/dot_general | solution.py:76
  125.1 2.7 copy.44
  127.9 4.7 convert_element_type.159
  132.6 6.5 convolution_convert_fusion.2
  140.7 63.8 %reduce-scatter.5.cloned.1.call-done = bf16[1176,768]{1,0:T(8,128)(2,1)} async-done(((bf16[4704,768]{1,0:T(8,128)(2,1)}), bf16[1176,768]{1,0:T(8,128)(2,1)}) %reduce-scatter.5.cloned.1.call-update) | async-done | bytes 1806352 | tf_op jit(solution)/shard_map/reduce_scatter | solution.py:82
  204.5 2.3 fusion.60
  207.1 4.9 multiply_reduce_fusion.2
  212.5 2.2 add_convert_fusion
  215.4 51.2 %all-gather.7.cloned.1.call-done = bf16[4704,768]{1,0:T(8,128)(2,1)} async-done(((bf16[1176,768]{1,0:T(8,128)(2,1)}), bf16[4704,768]{1,0:T(8,128)(2,1)}) %all-gather.7.cloned.1.call-update) | async-done | bytes 7225360 | tf_op jit(solution)/shard_map/all_gather | solution.py:93
  266.6 11.9 %fusion.74 = f32[4704,768]{1,0:T(8,128)} fusion(bf16[4704,768]{1,0:T(8,128)(2,1)} %all-gather.7.cloned.1.call-done, bf16[768,768]{1,0:T(8,128)(2,1)} %param.25), kind=kOutput, calls=%fused_computation.132 | convolution fusion | flops 5549064192 | bytes 22855680 | tf_op jit(solution)/shard_map/dot_general | solution.py:94
  278.5 41.8 %all-gather.9.cloned.1.call-done = bf16[4704,768]{1,0:T(8,128)(2,1)} async-done(((bf16[1176,768]{1,0:T(8,128)(2,1)}), bf16[4704,768]{1,0:T(8,128)(2,1)}) %all-gather.9.cloned.1.call-update) | async-done | bytes 7225360 | tf_op jit(solution)/shard_map/all_gather | solution.py:110
  320.3 41.0 %fusion.68 = (f32[768]{0:T(1024)S(1)}, bf16[4704,768]{1,0:T(8,128)(2,1)}, f32[4704,768]{1,0:T(8,128)S(1)}) fusion(f32[4704,768]{1,0:T(8,128)} %fusion.74, f32[768]{0:T(1024)S(1)} %copy-done.50, bf16[4704,768]{1,0:T(8,128)(2,1)} %all-gather.9.cloned.1.call-done, bf16[768,768]{1,0:T(8,128)(2,1)S(1)} %copy-done), kind=kOutput, calls=%fused_computation.128 | convolution fusion | flops 5816400896 | bytes 44537856 | tf_op jit(solution)/shard_map/td,fd->tf/dot_general | solution.py:112
  361.3 4.3 multiply_convert_fusion.1
  365.6 10.8 %convolution_convert_fusion.1 = bf16[4704,768]{1,0:T(8,128)(2,1)} fusion(bf16[4704,768]{1,0:T(8,128)(2,1)} %multiply_convert_fusion.1, bf16[768,768]{1,0:T(8,128)(2,1)S(1)} %copy-done), kind=kOutput, calls=%fused_computation.25 | convolution fusion | flops 5552676864 | bytes 15630336 | tf_op jit(solution)/shard_map/dot_general | solution.py:99
  377.7 11.2 %convolution_convert_fusion = bf16[4704,768]{1,0:T(8,128)(2,1)} fusion(bf16[768,768]{1,0:T(8,128)(2,1)S(1)} %copy-done.54, bf16[4704,768]{1,0:T(8,128)(2,1)} %get-tuple-element.43), kind=kOutput, calls=%fused_computation.24 | convolution fusion | flops 5552676864 | bytes 15630336 | tf_op jit(solution)/shard_map/tf,df->td/dot_general | solution.py:120
  389.1 52.8 %reduce-scatter.7.cloned.1.call-done = bf16[1176,768]{1,0:T(8,128)(2,1)} async-done(((bf16[4704,768]{1,0:T(8,128)(2,1)}), bf16[1176,768]{1,0:T(8,128)(2,1)}) %reduce-scatter.7.cloned.1.call-update) | async-done | bytes 1806352 | tf_op jit(solution)/shard_map/reduce_scatter | solution.py:98
  441.8 67.6 %reduce-scatter.9.cloned.1.call-done = bf16[1176,768]{1,0:T(8,128)(2,1)} async-done(((bf16[4704,768]{1,0:T(8,128)(2,1)}), bf16[1176,768]{1,0:T(8,128)(2,1)}) %reduce-scatter.9.cloned.1.call-update) | async-done | bytes 1806352 | tf_op jit(solution)/shard_map/reduce_scatter | solution.py:119
  509.5 8.3 fusion.36
  517.9 2.3 fusion.71
  520.2 1.8 copy-done.10
  523.5 51.8 %all-gather.11.cloned.1.call-done = bf16[4704,768]{1,0:T(8,128)(2,1)} async-done(((bf16[1176,768]{1,0:T(8,128)(2,1)}), bf16[4704,768]{1,0:T(8,128)(2,1)}) %all-gather.11.cloned.1.call-update) | async-done | bytes 7225360 | tf_op jit(solution)/shard_map/all_gather | solution.py:131
  575.3 6.8 convolution_convert_fusion.3
  582.1 6.2 reshape.193
  588.3 9.9 %convert_reduce_fusion.3 = (f32[3,64]{1,0:T(4,128)S(1)}, bf16[24,3,64,196]{3,2,1,0:T(8,128)(2,1)}) fusion(f32[24,3,196,196]{2,3,1,0:T(8,128)} %copy-done.2, f32[24,3,196]{2,1,0:T(4,128)S(1)} %copy-done.24, pred[24,196]{1,0:T(8,128)(4,1)S(1)} %copy-done.30, bf16[24,196,3,64]{1,0,3,2:T(8,128)(2,1)} %reshape.193), kind=kOutput, calls=%fused_computation.53 | convolution fusion | flops 367814976 | bytes 14738400 | tf_op jit(solution)/shard_map/ihqk,iqhd->ikhd/dot_general | solution.py:146
  599.8 11.2 %multiply_reduce_fusion = (f32[24,3,196]{2,1,0:T(4,128)S(1)}, f32[24,3,196,196]{2,3,1,0:T(8,128)}) fusion(f32[24,3,196,196]{2,3,1,0:T(8,128)S(1)} %bitcast.79, f32[24,3,196]{2,1,0:T(4,128)S(1)} %copy-done.24, pred[24,196]{1,0:T(8,128)(4,1)S(1)} %copy-done.30, f32[24,196,3,64]{1,0,3,2:T(8,128)} %squeeze.8, f32[3,64]{1,0:T(4,128)S(1)} %copy-done.47, ...), kind=kOutput, calls=%fused_computation.2 | convolution fusion | flops 369663840 | bytes 27664992 | tf_op jit(solution)/shard_map/iqhd,ikhd->ihqk/dot_general | solution.py:149
  611.0 10.2 %multiply_convert_fusion = bf16[24,3,196,196]{2,3,1,0:T(8,128)(2,1)} fusion(f32[24,3,196,196]{2,3,1,0:T(8,128)} %get-tuple-element.59, f32[24,3,196,196]{2,3,1,0:T(8,128)S(1)} %bitcast.79, f32[24,3,196]{2,1,0:T(4,128)S(1)} %get-tuple-element.58, f32[24,3,196]{2,1,0:T(4,128)S(1)} %copy-done.24, pred[24,196]{1,0:T(8,128)(4,1)S(1)} %copy-done.30), kind=kLoop, calls=%fused_computation.1 | loop fusion | flops 16595712 | bytes 27777120 | tf_op jit(solution)/shard_map/convert_element_type | solution.py:153
  621.2 8.7 fusion.43
  630.0 2.9 convert_reduce_fusion.4
  632.9 2.8 copy.53
  635.7 4.7 convert_element_type.185
  640.5 2.7 copy.48
  643.2 4.7 convert_element_type.179
  647.9 3.0 copy.50
  650.9 3.0 convert_element_type.182
  654.0 1.8 constant_dynamic-update-slice_fusion.2
  656.8 2.3 copy-done.26
  659.1 7.9 bitcast_convert_fusion
  667.1 11.8 %fusion.38 = f32[768,768]{1,0:T(8,128)} fusion(bf16[4704,768]{1,0:T(8,128)(2,1)} %all-gather.7.cloned.1.call-done, bf16[4704,768]{1,0:T(8,128)(2,1)} %get-tuple-element.43), kind=kOutput, calls=%fused_computation.78 | convolution fusion | flops 5549064192 | bytes 16809984 | tf_op jit(solution)/shard_map/td,tf->df/dot_general | solution.py:117
  678.9 12.2 %fusion.76 = f32[768,768]{1,0:T(8,128)} fusion(bf16[4704,768]{1,0:T(8,128)(2,1)} %multiply_convert_fusion.1, bf16[4704,768]{1,0:T(8,128)(2,1)} %all-gather.9.cloned.1.call-done), kind=kOutput, calls=%fused_computation.134 | convolution fusion | flops 5549064192 | bytes 16809984 | tf_op jit(solution)/shard_map/tf,td->fd/dot_general | solution.py:111
  691.1 2.5 fusion.75
  693.6 5.9 fusion.8
  699.6 2.8 pad_maximum_fusion.1
  702.6 22.3 %all-reduce.1 = (f32[2,192]{1,0:T(2,128)}, f32[768]{0:T(1024)}) all-reduce(f32[2,192]{1,0:T(2,128)S(1)} %pad_maximum_fusion, f32[768]{0:T(1024)S(1)} %get-tuple-element.42), channel_id=1, replica_groups=mesh['dp'=8,'tensor'=4] {'dp'}, use_global_device_ids=true, to_apply=%region_22.23 | all-reduce | flops 1152 | bytes 9216 | tf_op jit(solution)/shard_map/psum | solution.py:205
  724.8 7.6 reduce-scatter.11.cloned.1.call-done
  732.4 3.4 fusion.37
  735.8 44.5 %all-reduce = (f32[768]{0:T(1024)}, f32[768]{0:T(1024)}, f32[768]{0:T(1024)}, f32[768]{0:T(1024)}, f32[768]{0:T(1024)}, /*index=5*/f32[768]{0:T(1024)}, f32[4]{0:T(128)S(1)}) all-reduce(f32[768]{0:T(1024)S(1)} %get-tuple-element.17, f32[768]{0:T(1024)S(1)} %get-tuple-element.25, ...), channel_id=1, replica_groups=mesh['dp'=8,'tensor'=4] {'dp','tensor'}, use_global_device_ids=true, to_apply=%region_16.17 | all-reduce | flops 4612 | bytes 36896 | tf_op jit(solution)/shard_map/psum | solution.py:193
  782.1 4.6 fusion.29
  786.7 183.9 %all-reduce.5.cloned.1.call-done = (f32[768,3,192]{0,2,1:T(8,128)}, f32[192,768]{1,0:T(8,128)}, f32[768,768]{1,0:T(8,128)}, f32[768,768]{1,0:T(8,128)}) async-done(((f32[768,3,192]{0,2,1:T(8,128)}, f32[192,768]{1,0:T(8,128)}, f32[768,768]{1,0:T(8,128)}, f32[768,768]{1,0:T(8,128)}), (f32[768,3,192]{0,2,1:T(8,128)}, f32[192,768]{1,0:T(8,128)}, f32[768,768]{1,0:T(8,128)}, ...) | async-done | bytes 7077904 | tf_op jit(solution)/shard_map/psum | solution.py:205
  970.6 2.9 copy.96
  973.6 2.0 copy.97
  975.6 1.4 copy.98
  977.0 1.4 copy.99
  (178 shorter events, 14.3 us)
Async XLA Ops:
  7.2 313.1 %copy-start = (bf16[768,768]{1,0:T(8,128)(2,1)S(1)}, bf16[768,768]{1,0:T(8,128)(2,1)}, u32[]{:S(2)}) copy-start(bf16[768,768]{1,0:T(8,128)(2,1)} %param.27) | copy-start | bytes 3538948
  7.2 4.8 copy-start.3
  7.2 7.5 copy-start.53
  7.2 8.9 copy-start.56
  7.2 62.0 %all-gather.5.cloned.1.call-start = ((), (), s32[]{:S(2)}) async-start(), calls=%async_computation.4 | async-start | bytes 9031680 | tf_op jit(solution)/shard_map/all_gather | solution.py:66
  14.7 189.8 %reduce-scatter.5.cloned.1.call-start = ((), (), s32[]{:S(2)}) async-start(), calls=%async_computation.5 | async-start | bytes 9031680 | tf_op jit(solution)/shard_map/reduce_scatter | solution.py:82
  16.8 97.2 %copy-start.29 = (pred[24,196]{1,0:T(8,128)(4,1)}, pred[24,196]{1,0:T(8,128)(4,1)S(1)}, u32[]{:S(2)}) copy-start(pred[24,196]{1,0:T(8,128)(4,1)S(1)} %get-tuple-element.54) | copy-start | bytes 14116
  107.7 5.3 copy-start.2
  114.0 11.1 %copy-start.23 = (f32[24,3,196]{2,1,0:T(4,128)}, f32[24,3,196]{2,1,0:T(4,128)S(1)}, u32[]{:S(2)}) copy-start(f32[24,3,196]{2,1,0:T(4,128)S(1)} %log_add_fusion) | copy-start | bytes 169348
  125.1 7.5 copy-start.27
  139.1 65.4 %copy-start.41 = (f32[768]{0:T(1024)S(1)}, f32[768]{0:T(1024)}, u32[]{:S(2)}) copy-start(f32[768]{0:T(1024)} %param.22) | copy-start | bytes 9220
  139.1 127.5 %all-gather.7.cloned.1.call-start = ((), (), s32[]{:S(2)}) async-start(), calls=%async_computation.6 | async-start | bytes 9031680 | tf_op jit(solution)/shard_map/all_gather | solution.py:93
  140.7 71.3 %copy-start.37 = (f32[1176]{0:T(1024)}, f32[1176]{0:T(1024)S(1)}, u32[]{:S(2)}) copy-start(f32[1176]{0:T(1024)S(1)} %get-tuple-element.46) | copy-start | bytes 14116
  140.7 71.9 %copy-start.44 = (f32[768]{0:T(1024)S(1)}, f32[768]{0:T(1024)}, u32[]{:S(2)}) copy-start(f32[768]{0:T(1024)} %param.23) | copy-start | bytes 9220
  140.7 71.9 %copy-start.52 = (f32[768]{0:T(1024)S(1)}, f32[768]{0:T(1024)}, u32[]{:S(2)}) copy-start(f32[768]{0:T(1024)} %param.24) | copy-start | bytes 9220
  206.8 5.1 copy-start.33
  214.8 105.5 %all-gather.9.cloned.1.call-start = ((), (), s32[]{:S(2)}) async-start(), calls=%async_computation.8 | async-start | bytes 9031680 | tf_op jit(solution)/shard_map/all_gather | solution.py:110
  215.4 104.9 %copy-start.50 = (f32[768]{0:T(1024)S(1)}, f32[768]{0:T(1024)}, u32[]{:S(2)}) copy-start(f32[768]{0:T(1024)} %param.26) | copy-start | bytes 9220
  215.4 226.5 %reduce-scatter.7.cloned.1.call-start = ((), (), s32[]{:S(2)}) async-start(), calls=%async_computation.7 | async-start | bytes 9031680 | tf_op jit(solution)/shard_map/reduce_scatter | solution.py:98
  320.3 41.1 %copy-start.13 = (f32[4704,768]{1,0:T(8,128)S(1)}, f32[4704,768]{1,0:T(8,128)}, u32[]{:S(2)}) copy-start(f32[4704,768]{1,0:T(8,128)} %fusion.74) | copy-start | bytes 43352068
  376.5 133.0 %reduce-scatter.9.cloned.1.call-start = ((), (), s32[]{:S(2)}) async-start(), calls=%async_computation.9 | async-start | bytes 9031680 | tf_op jit(solution)/shard_map/reduce_scatter | solution.py:119
  389.0 120.5 %copy-start.4 = (bf16[1176,768]{1,0:T(8,128)(2,1)S(1)}, bf16[1176,768]{1,0:T(8,128)(2,1)}, u32[]{:S(2)}) copy-start(bf16[1176,768]{1,0:T(8,128)(2,1)} %param.15) | copy-start | bytes 5419012
  389.0 120.5 %copy-start.34 = (f32[1176]{0:T(1024)S(1)}, f32[1176]{0:T(1024)}, u32[]{:S(2)}) copy-start(f32[1176]{0:T(1024)} %copy-done.33) | copy-start | bytes 14116
  389.0 120.5 %copy-start.38 = (f32[1176]{0:T(1024)S(1)}, f32[1176]{0:T(1024)}, u32[]{:S(2)}) copy-start(f32[1176]{0:T(1024)} %copy-done.37) | copy-start | bytes 14116
  389.0 120.5 %copy-start.40 = (f32[1176]{0:T(1024)S(1)}, f32[1176]{0:T(1024)}, u32[]{:S(2)}) copy-start(f32[1176]{0:T(1024)} %copy-done.39) | copy-start | bytes 14116
  389.0 120.5 %copy-start.42 = (f32[768]{0:T(1024)S(1)}, f32[768]{0:T(1024)}, u32[]{:S(2)}) copy-start(f32[768]{0:T(1024)} %param.22) | copy-start | bytes 9220
  389.0 120.5 %copy-start.45 = (f32[768]{0:T(1024)S(1)}, f32[768]{0:T(1024)}, u32[]{:S(2)}) copy-start(f32[768]{0:T(1024)} %param.23) | copy-start | bytes 9220
  389.0 120.5 %copy-start.51 = (f32[768]{0:T(1024)S(1)}, f32[768]{0:T(1024)}, u32[]{:S(2)}) copy-start(f32[768]{0:T(1024)} %param.28) | copy-start | bytes 9220
  389.0 186.2 %all-gather.11.cloned.1.call-start = ((), (), s32[]{:S(2)}) async-start(), calls=%async_computation.10 | async-start | bytes 9031680 | tf_op jit(solution)/shard_map/all_gather | solution.py:131
  509.5 8.3 copy-start.8
  509.5 8.3 copy-start.18
  509.5 8.3 copy-start.19
  520.2 55.1 %copy-start.28 = (bf16[192,768]{1,0:T(8,128)(2,1)S(1)}, bf16[192,768]{1,0:T(8,128)(2,1)}, u32[]{:S(2)}) copy-start(bf16[192,768]{1,0:T(8,128)(2,1)} %param.21) | copy-start | bytes 884740
  523.4 64.8 %copy-start.24 = (f32[24,3,196]{2,1,0:T(4,128)S(1)}, f32[24,3,196]{2,1,0:T(4,128)}, u32[]{:S(2)}) copy-start(f32[24,3,196]{2,1,0:T(4,128)} %copy-done.23) | copy-start | bytes 169348
  523.5 64.8 %copy-start.30 = (pred[24,196]{1,0:T(8,128)(4,1)S(1)}, pred[24,196]{1,0:T(8,128)(4,1)}, u32[]{:S(2)}) copy-start(pred[24,196]{1,0:T(8,128)(4,1)} %copy-done.29) | copy-start | bytes 14116
  523.5 208.9 %reduce-scatter.11.cloned.1.call-start = ((), (), s32[]{:S(2)}) async-start(), calls=%async_computation.11 | async-start | bytes 9031680 | tf_op jit(solution)/shard_map/reduce_scatter | solution.py:174
  582.1 16.2 %slice-start = ((s8[14745600]{0:T(1024)(128)(4,1)}), s8[2162688]{0:T(1024)(128)(4,1)S(1)}, s32[]{:S(2)}) async-start(s8[14745600]{0:T(1024)(128)(4,1)} %bitcast.78), calls=%async_computation.13 | async-start | bytes 4325376
  588.3 10.0 %slice-start.1 = ((s8[14745600]{0:T(1024)(128)(4,1)}), s8[4194304]{0:T(1024)(128)(4,1)S(1)}, s32[]{:S(2)}) async-start(s8[14745600]{0:T(1024)(128)(4,1)} %bitcast.78), calls=%async_computation.14 | async-start | bytes 8388608
  588.3 10.0 %slice-start.2 = ((s8[14745600]{0:T(1024)(128)(4,1)}), s8[4194304]{0:T(1024)(128)(4,1)S(1)}, s32[]{:S(2)}) async-start(s8[14745600]{0:T(1024)(128)(4,1)} %bitcast.78), calls=%async_computation.15 | async-start | bytes 8388608
  588.3 10.9 %slice-start.3 = ((s8[14745600]{0:T(1024)(128)(4,1)}), s8[4194304]{0:T(1024)(128)(4,1)S(1)}, s32[]{:S(2)}) async-start(s8[14745600]{0:T(1024)(128)(4,1)} %bitcast.78), calls=%async_computation.16 | async-start | bytes 8388608
  588.3 11.5 %copy-start.11 = (bf16[24,196,3,64]{1,0,3,2:T(8,128)(2,1)S(1)}, bf16[24,196,3,64]{1,0,3,2:T(8,128)(2,1)}, u32[]{:S(2)}) copy-start(bf16[24,196,3,64]{1,0,3,2:T(8,128)(2,1)} %reshape.193) | copy-start | bytes 5419012
  588.3 11.5 %copy-start.47 = (f32[3,64]{1,0:T(4,128)S(1)}, f32[3,64]{1,0:T(4,128)}, u32[]{:S(2)}) copy-start(f32[3,64]{1,0:T(4,128)} %add.138) | copy-start | bytes 2308
  611.0 10.2 %copy-start.48 = (f32[3,64]{1,0:T(4,128)S(1)}, f32[3,64]{1,0:T(4,128)}, u32[]{:S(2)}) copy-start(f32[3,64]{1,0:T(4,128)} %add.141) | copy-start | bytes 2308
  621.2 8.8 copy-start.6
  621.2 8.8 copy-start.9
  630.0 2.9 copy-start.22
  632.9 7.6 copy-start.12
  654.0 5.1 copy-start.55
  667.1 303.6 %all-reduce.5.cloned.1.call-start = ((), (), s32[]{:S(2)}) async-start(), calls=%async_computation.12 | async-start | bytes 14155776 | tf_op jit(solution)/shard_map/psum | solution.py:205
  667.1 24.0 %slice-start.8 = ((s8[7225344]{0:T(1024)(128)(4,1)}), s8[4194304]{0:T(1024)(128)(4,1)S(1)}, s32[]{:S(2)}) async-start(s8[7225344]{0:T(1024)(128)(4,1)} %bitcast.86), calls=%async_computation.21 | async-start | bytes 8388608
  667.1 26.5 %slice-start.4 = ((s8[5455872]{0:T(1024)(128)(4,1)}), s8[4194304]{0:T(1024)(128)(4,1)S(1)}, s32[]{:S(2)}) async-start(s8[5455872]{0:T(1024)(128)(4,1)} %bitcast.82), calls=%async_computation.17 | async-start | bytes 8388608
  667.1 26.5 %slice-start.6 = ((s8[7225344]{0:T(1024)(128)(4,1)}), s8[4194304]{0:T(1024)(128)(4,1)S(1)}, s32[]{:S(2)}) async-start(s8[7225344]{0:T(1024)(128)(4,1)} %bitcast.84), calls=%async_computation.19 | async-start | bytes 8388608
  678.9 12.2 %copy-start.14 = (bf16[4704,192]{0,1:T(8,128)(2,1)S(1)}, bf16[4704,192]{0,1:T(8,128)(2,1)}, u32[]{:S(2)}) copy-start(bf16[4704,192]{0,1:T(8,128)(2,1)} %convert_element_type.159) | copy-start | bytes 5419012
  678.9 12.2 %slice-start.9 = ((s8[7225344]{0:T(1024)(128)(4,1)}), s8[3031040]{0:T(1024)(128)(4,1)S(1)}, s32[]{:S(2)}) async-start(s8[7225344]{0:T(1024)(128)(4,1)} %bitcast.86), calls=%async_computation.22 | async-start | bytes 6062080
  678.9 14.7 %slice-start.5 = ((s8[5455872]{0:T(1024)(128)(4,1)}), s8[1261568]{0:T(1024)(128)(4,1)S(1)}, s32[]{:S(2)}) async-start(s8[5455872]{0:T(1024)(128)(4,1)} %bitcast.82), calls=%async_computation.18 | async-start | bytes 2523136
  678.9 14.7 %slice-start.7 = ((s8[7225344]{0:T(1024)(128)(4,1)}), s8[3031040]{0:T(1024)(128)(4,1)S(1)}, s32[]{:S(2)}) async-start(s8[7225344]{0:T(1024)(128)(4,1)} %bitcast.84), calls=%async_computation.20 | async-start | bytes 6062080
  699.5 32.8 %copy-start.5 = (bf16[1176,768]{1,0:T(8,128)(2,1)S(1)}, bf16[1176,768]{1,0:T(8,128)(2,1)}, u32[]{:S(2)}) copy-start(bf16[1176,768]{1,0:T(8,128)(2,1)} %param.15) | copy-start | bytes 5419012
  699.5 32.8 %copy-start.32 = (f32[1176]{0:T(1024)S(1)}, f32[1176]{0:T(1024)}, u32[]{:S(2)}) copy-start(f32[1176]{0:T(1024)} %copy-done.31) | copy-start | bytes 14116
  699.5 32.8 %copy-start.36 = (f32[1176]{0:T(1024)S(1)}, f32[1176]{0:T(1024)}, u32[]{:S(2)}) copy-start(f32[1176]{0:T(1024)} %copy-done.35) | copy-start | bytes 14116
  699.6 32.8 %copy-start.46 = (f32[768]{0:T(1024)S(1)}, f32[768]{0:T(1024)}, u32[]{:S(2)}) copy-start(f32[768]{0:T(1024)} %param.17) | copy-start | bytes 9220
  699.6 36.3 %copy-start.49 = (f32[768]{0:T(1024)S(1)}, f32[768]{0:T(1024)}, u32[]{:S(2)}) copy-start(f32[768]{0:T(1024)} %get-tuple-element.26) | copy-start | bytes 9220
  970.6 5.0 copy-start.21
  970.6 6.4 copy-start.20
  973.6 4.8 copy-start.1
  (12 other events, 19.7 us)
Sparse Core Ops, SparseCore 0:
  14.8 54.3 all-gather.4
  139.3 65.1 reduce-scatter.4
  214.9 51.6 all-gather.6
  268.6 51.6 all-gather.8
  376.6 65.1 reduce-scatter.6
  444.3 65.1 reduce-scatter.8
  523.6 51.6 all-gather.10
  667.2 65.1 reduce-scatter.10
  738.0 232.6 all-reduce.4
where the time goes:
time: 995 us; the launch traced here: 985 us
  waiting for transfers between devices  574 us (58%)
  matrix products  187 us (19%)
  local copies, waits for them, and re-layouts  81.1 us (8%)
  blocking collectives  66.7 us (7%)
  other arithmetic  61.1 us (6%)
  between operations  15.5 us (2%)
    psum x1, waiting for transfers between devices, on_device(): lax.psum((weight_qkv, grad_bias_qv, weight_out, weight_up, grad_bias_up,...  184 us
    reduce_scatter x1, waiting for transfers between devices, on_device(): lax.psum_scatter(jnp.einsum('tf,df->td', piece, w_up, preferred_element_t...  67.6 us
    reduce_scatter x1, waiting for transfers between devices, on_device(): lax.psum_scatter(jnp.dot(piece, w_out, preferred_element_type=jnp.float32...  63.8 us
    reduce_scatter x1, waiting for transfers between devices, on_device(): lax.psum_scatter(jnp.dot(piece, w_down, preferred_element_type=jnp.float3...  52.8 us
    all_gather x1, waiting for transfers between devices, on_device(): full_attn = lax.all_gather(in_attn, 'tensor', axis=0, tiled=True)  52.4 us
    all_gather x1, waiting for transfers between devices, on_device(): lax.all_gather(grad_hidden.astype(jnp.bfloat16), 'tensor', axis=0, tiled=...  51.8 us
    all_gather x1, waiting for transfers between devices, on_device(): full_mlp = lax.all_gather(in_mlp, 'tensor', axis=0, tiled=True)  51.2 us
    psum x1, blocking collectives, on_device(): lax.psum((grad_gain_attn, grad_shift_attn, grad_bias_out, grad_gain_mlp,...  44.5 us
  transfers between devices with their start and end apart: 9, of which 9 were waited for; matrix products, arithmetic and copies ran while one was open for 7% of the time, Pallas kernels for 0%

commit v1 on v0

--- a/solution.py
+++ b/solution.py
@@ -90,7 +90,16 @@
     hidden = inputs + branch
     normed_m, factor_m = normalize(hidden)
     in_mlp = (normed_m * gain_mlp + shift_mlp).astype(jnp.bfloat16)
-    full_mlp = lax.all_gather(in_mlp, "tensor", axis=0, tiled=True)
+    peers, index, width_2 = (lax.axis_size("tensor"), lax.axis_index("tensor"), in_mlp.shape[0])
+    upward = [(i, (i + 1) % peers) for i in range(peers)]
+    whole = jnp.zeros((*in_mlp.shape[:0], peers * width_2, *in_mlp.shape[0 + 1 :]), in_mlp.dtype)
+    carried = in_mlp
+    for step in range(peers):
+        owner = (index - step) % peers
+        whole = lax.dynamic_update_slice_in_dim(whole, carried, owner * width_2, axis=0)
+        if step < peers - 1:
+            carried = lax.ppermute(carried, "tensor", upward)
+    full_mlp = whole
     pre_act = jnp.dot(full_mlp, w_up, preferred_element_type=jnp.float32) + bias_up
     act = exact_gelu(pre_act).astype(jnp.bfloat16)
     piece = act

time: 995 us -> 1020 us (1.025)
  starting transfers between devices: 0.37 us -> 12.1 us
  local copies, waits for them, and re-layouts: 81.1 us -> 92.3 us
    ppermute x0 -> x3, waiting for transfers between devices: none -> 93.2 us  [on_device(): carried = lax.ppermute(carried, 'tensor', upward)]
    all_gather x1 -> x0, waiting for transfers between devices: 51.2 us -> none  [on_device(): full_mlp = lax.all_gather(in_mlp, 'tensor', axis=0, tiled=True)]
    all_gather x1, waiting for transfers between devices: 41.8 us -> 0.01 us  [on_device(): lax.all_gather(grad_stream.astype(jnp.bfloat16), 'tensor', axis=0, tiled=...]
    reduce_scatter x1, starting transfers between devices: 0.04 us -> 11.4 us  [on_device(): lax.psum_scatter(jnp.dot(piece, w_down, preferred_element_type=jnp.float3...]
    unnamed x140 -> x146, local copies, waits for them, and re-layouts: 20.2 us -> 23.8 us
  transfers between devices with their start and end apart: 9 -> 11, of which waited for: 9 -> 10; matrix products, arithmetic and copies ran while one was open for 7% -> 8% of each run, Pallas kernels for 0% -> 0%
where the time goes in v1:
time: 1020 us; the launch traced here: 1010 us
  waiting for transfers between devices  573 us (56%)
  matrix products  186 us (18%)
  local copies, waits for them, and re-layouts  92.3 us (9%)
  blocking collectives  66.7 us (7%)
  other arithmetic  59.6 us (6%)
  between operations  15.9 us (2%)
  starting transfers between devices  12.1 us (1%)
    psum x1, waiting for transfers between devices, on_device(): lax.psum((weight_qkv, grad_bias_qv, weight_out, weight_up, grad_bias_up,...  184 us
    ppermute x3, waiting for transfers between devices, on_device(): carried = lax.ppermute(carried, 'tensor', upward)  93.2 us
    reduce_scatter x1, waiting for transfers between devices, on_device(): lax.psum_scatter(jnp.einsum('tf,df->td', piece, w_up, preferred_element_t...  67.6 us
    reduce_scatter x1, waiting for transfers between devices, on_device(): lax.psum_scatter(jnp.dot(piece, w_out, preferred_element_type=jnp.float32...  63.8 us
    reduce_scatter x1, waiting for transfers between devices, on_device(): lax.psum_scatter(jnp.dot(piece, w_down, preferred_element_type=jnp.float3...  53.1 us
    all_gather x1, waiting for transfers between devices, on_device(): full_attn = lax.all_gather(in_attn, 'tensor', axis=0, tiled=True)  52.4 us
    all_gather x1, waiting for transfers between devices, on_device(): lax.all_gather(grad_hidden.astype(jnp.bfloat16), 'tensor', axis=0, tiled=...  51.3 us
    psum x1, blocking collectives, on_device(): lax.psum((grad_gain_attn, grad_shift_attn, grad_bias_out, grad_gain_mlp,...  44.5 us
  transfers between devices with their start and end apart: 11, of which 10 were waited for; matrix products, arithmetic and copies ran while one was open for 8% of the time, Pallas kernels for 0%

profile of v1, /device:TPU:0, one launch (start us, length us, event | category | flops | bytes accessed | tf_op | source)
XLA Modules:
  0.0 1006.3 jit_solution(2038117565669979429)
XLA Ops:
  7.3 2.0 convert_reduce_fusion.2
  9.2 2.1 fusion.30
  12.0 2.6 fusion.26
  16.8 52.4 %all-gather.4.cloned.1.call-done = bf16[4704,768]{1,0:T(8,128)(2,1)} async-done(((bf16[1176,768]{1,0:T(8,128)(2,1)}), bf16[4704,768]{1,0:T(8,128)(2,1)}) %all-gather.4.cloned.1.call-update) | async-done | bytes 7225360 | tf_op jit(solution)/shard_map/all_gather | solution.py:66
  69.2 7.3 fusion.10
  77.9 3.5 fusion.73
  81.4 6.0 convert_element_type.155
  87.4 6.4 squeeze.9
  93.9 6.4 squeeze.8
  100.3 7.4 fusion.6
  108.3 4.5 exponential_reduce_fusion
  113.9 11.1 %convert_bitcast_fusion = bf16[24,196,3,64]{1,3,2,0:T(8,128)(2,1)S(1)} fusion(f32[24,196,3,64]{1,0,3,2:T(8,128)} %squeeze.8, f32[3,64]{1,0:T(4,128)} %add.166, f32[24,3,196,196]{2,3,1,0:T(8,128)} %copy-done.2, f32[24,3,196]{2,1,0:T(4,128)S(1)} %log_add_fusion, pred[24,196]{1,0:T(8,128)(4,1)S(1)} %get-tuple-element.56), kind=kOutput, calls=%fused_computation.91 | convolution fusion | flops 367815168 | bytes 16544736 | tf_op jit(solution)/shard_map/ihqk,ikhd->iqhd/dot_general | solution.py:76
  125.0 2.7 copy.44
  127.8 4.7 convert_element_type.159
  132.5 6.5 convolution_convert_fusion.2
  140.5 63.8 %reduce-scatter.5.cloned.1.call-done = bf16[1176,768]{1,0:T(8,128)(2,1)} async-done(((bf16[4704,768]{1,0:T(8,128)(2,1)}), bf16[1176,768]{1,0:T(8,128)(2,1)}) %reduce-scatter.5.cloned.1.call-update) | async-done | bytes 1806352 | tf_op jit(solution)/shard_map/reduce_scatter | solution.py:82
  204.4 2.3 fusion.60
  206.9 4.7 multiply_reduce_fusion.2
  211.6 11.4 %reduce-scatter.7.cloned.1.call-start = ((), (), s32[]{:S(2)}) async-start(), calls=%async_computation.6 | async-start | bytes 9031680 | tf_op jit(solution)/shard_map/reduce_scatter | solution.py:107
  225.8 2.9 copy-done.21
  228.7 52.3 %collective-permute-done = bf16[1176,768]{1,0:T(8,128)(2,1)S(1)} collective-permute-done((bf16[1176,768]{1,0:T(8,128)(2,1)S(1)}, bf16[1176,768]{1,0:T(8,128)(2,1)S(1)}, u32[]{:S(2)}, u32[]{:S(2)}) %collective-permute-start) | collective-permute-done | bytes 1806368 | tf_op jit(solution)/shard_map/ppermute | solution.py:101
  281.1 22.4 %collective-permute-done.1 = bf16[1176,768]{1,0:T(8,128)(2,1)} collective-permute-done((bf16[1176,768]{1,0:T(8,128)(2,1)S(1)}, bf16[1176,768]{1,0:T(8,128)(2,1)}, u32[]{:S(2)}, u32[]{:S(2)}) %collective-permute-start.1) | collective-permute-done | bytes 1806368 | tf_op jit(solution)/shard_map/ppermute | solution.py:101
  304.9 2.8 constant_dynamic-update-slice_fusion.4
  307.7 18.4 %collective-permute-done.2 = bf16[1176,768]{1,0:T(8,128)(2,1)} collective-permute-done((bf16[1176,768]{1,0:T(8,128)(2,1)}, bf16[1176,768]{1,0:T(8,128)(2,1)}, u32[]{:S(2)}, u32[]{:S(2)}) %collective-permute-start.2) | collective-permute-done | bytes 1806368 | tf_op jit(solution)/shard_map/ppermute | solution.py:101
  326.2 2.8 constant_dynamic-update-slice_fusion.3
  329.0 11.6 %fusion.74 = f32[4704,768]{1,0:T(8,128)} fusion(bf16[4704,768]{1,0:T(8,128)(2,1)} %constant_dynamic-update-slice_fusion.3, bf16[768,768]{1,0:T(8,128)(2,1)S(1)} %copy-done.56), kind=kOutput, calls=%fused_computation.136 | convolution fusion | flops 5549064192 | bytes 22855680 | tf_op jit(solution)/shard_map/dot_general | solution.py:103
  340.7 41.1 %fusion.68 = (f32[768]{0:T(1024)S(1)}, bf16[4704,768]{1,0:T(8,128)(2,1)}, f32[4704,768]{1,0:T(8,128)S(1)}) fusion(f32[4704,768]{1,0:T(8,128)} %fusion.74, f32[768]{0:T(1024)S(1)} %copy-done.53, bf16[4704,768]{1,0:T(8,128)(2,1)} %all-gather.6.cloned.1.call-done, bf16[768,768]{1,0:T(8,128)(2,1)S(1)} %copy-done), kind=kOutput, calls=%fused_computation.132 | convolution fusion | flops 5816400896 | bytes 44537856 | tf_op jit(solution)/shard_map/td,fd->tf/dot_general | solution.py:121
  381.8 4.4 multiply_convert_fusion.1
  386.1 10.8 %convolution_convert_fusion.1 = bf16[4704,768]{1,0:T(8,128)(2,1)} fusion(bf16[4704,768]{1,0:T(8,128)(2,1)} %multiply_convert_fusion.1, bf16[768,768]{1,0:T(8,128)(2,1)S(1)} %copy-done), kind=kOutput, calls=%fused_computation.25 | convolution fusion | flops 5552676864 | bytes 15630336 | tf_op jit(solution)/shard_map/dot_general | solution.py:108
  398.2 10.8 %convolution_convert_fusion = bf16[4704,768]{1,0:T(8,128)(2,1)} fusion(bf16[768,768]{1,0:T(8,128)(2,1)S(1)} %copy-done.57, bf16[4704,768]{1,0:T(8,128)(2,1)} %get-tuple-element.43), kind=kOutput, calls=%fused_computation.24 | convolution fusion | flops 5552676864 | bytes 15630336 | tf_op jit(solution)/shard_map/tf,df->td/dot_general | solution.py:129
  409.2 53.1 %reduce-scatter.7.cloned.1.call-done = bf16[1176,768]{1,0:T(8,128)(2,1)} async-done(((bf16[4704,768]{1,0:T(8,128)(2,1)}), bf16[1176,768]{1,0:T(8,128)(2,1)}) %reduce-scatter.7.cloned.1.call-update) | async-done | bytes 1806352 | tf_op jit(solution)/shard_map/reduce_scatter | solution.py:107
  462.3 67.6 %reduce-scatter.9.cloned.1.call-done = bf16[1176,768]{1,0:T(8,128)(2,1)} async-done(((bf16[4704,768]{1,0:T(8,128)(2,1)}), bf16[1176,768]{1,0:T(8,128)(2,1)}) %reduce-scatter.9.cloned.1.call-update) | async-done | bytes 1806352 | tf_op jit(solution)/shard_map/reduce_scatter | solution.py:128
  530.0 8.3 fusion.36
  538.3 2.3 fusion.71
  540.7 1.8 copy-done.11
  544.4 51.3 %all-gather.8.cloned.1.call-done = bf16[4704,768]{1,0:T(8,128)(2,1)} async-done(((bf16[1176,768]{1,0:T(8,128)(2,1)}), bf16[4704,768]{1,0:T(8,128)(2,1)}) %all-gather.8.cloned.1.call-update) | async-done | bytes 7225360 | tf_op jit(solution)/shard_map/all_gather | solution.py:140
  595.7 6.8 convolution_convert_fusion.3
  602.5 6.2 reshape.193
  608.7 9.9 convert_reduce_fusion.3
  620.3 11.3 %multiply_reduce_fusion = (f32[24,3,196]{2,1,0:T(4,128)S(1)}, f32[24,3,196,196]{2,3,1,0:T(8,128)}) fusion(f32[24,3,196,196]{2,3,1,0:T(8,128)S(1)} %bitcast.79, f32[24,3,196]{2,1,0:T(4,128)S(1)} %copy-done.26, pred[24,196]{1,0:T(8,128)(4,1)S(1)} %copy-done.32, f32[24,196,3,64]{1,0,3,2:T(8,128)} %squeeze.8, f32[3,64]{1,0:T(4,128)S(1)} %copy-done.49, ...), kind=kOutput, calls=%fused_computation.2 | convolution fusion | flops 369663840 | bytes 27664992 | tf_op jit(solution)/shard_map/iqhd,ikhd->ihqk/dot_general | solution.py:158
  631.5 10.2 %multiply_convert_fusion = bf16[24,3,196,196]{2,3,1,0:T(8,128)(2,1)} fusion(f32[24,3,196,196]{2,3,1,0:T(8,128)} %get-tuple-element.61, f32[24,3,196,196]{2,3,1,0:T(8,128)S(1)} %bitcast.79, f32[24,3,196]{2,1,0:T(4,128)S(1)} %get-tuple-element.60, f32[24,3,196]{2,1,0:T(4,128)S(1)} %copy-done.26, pred[24,196]{1,0:T(8,128)(4,1)S(1)} %copy-done.32), kind=kLoop, calls=%fused_computation.1 | loop fusion | flops 16595712 | bytes 27777120 | tf_op jit(solution)/shard_map/convert_element_type | solution.py:162
  641.8 8.7 fusion.43
  650.5 2.9 convert_reduce_fusion.4
  653.5 2.8 copy.53
  656.3 4.7 convert_element_type.185
  661.0 2.7 copy.48
  663.8 4.7 convert_element_type.179
  668.5 3.0 copy.50
  671.5 3.0 convert_element_type.182
  677.4 2.4 copy-done.28
  679.8 7.9 bitcast_convert_fusion
  687.8 11.8 %fusion.38 = f32[768,768]{1,0:T(8,128)} fusion(bf16[4704,768]{1,0:T(8,128)(2,1)} %constant_dynamic-update-slice_fusion.3, bf16[4704,768]{1,0:T(8,128)(2,1)} %get-tuple-element.43), kind=kOutput, calls=%fused_computation.78 | convolution fusion | flops 5549064192 | bytes 16809984 | tf_op jit(solution)/shard_map/td,tf->df/dot_general | solution.py:126
  699.6 12.2 %fusion.76 = f32[768,768]{1,0:T(8,128)} fusion(bf16[4704,768]{1,0:T(8,128)(2,1)} %multiply_convert_fusion.1, bf16[4704,768]{1,0:T(8,128)(2,1)} %all-gather.6.cloned.1.call-done), kind=kOutput, calls=%fused_computation.138 | convolution fusion | flops 5549064192 | bytes 16809984 | tf_op jit(solution)/shard_map/tf,td->fd/dot_general | solution.py:120
  711.8 2.5 fusion.75
  714.3 5.9 fusion.8
  720.3 2.8 pad_maximum_fusion.1
  723.3 22.3 %all-reduce.1 = (f32[2,192]{1,0:T(2,128)}, f32[768]{0:T(1024)}) all-reduce(f32[2,192]{1,0:T(2,128)S(1)} %pad_maximum_fusion, f32[768]{0:T(1024)S(1)} %get-tuple-element.42), channel_id=1, replica_groups=mesh['dp'=8,'tensor'=4] {'dp'}, use_global_device_ids=true, to_apply=%region_22.23 | all-reduce | flops 1152 | bytes 9216 | tf_op jit(solution)/shard_map/psum | solution.py:214
  745.5 7.6 reduce-scatter.11.cloned.1.call-done
  753.1 3.4 fusion.37
  756.5 44.5 %all-reduce = (f32[768]{0:T(1024)}, f32[768]{0:T(1024)}, f32[768]{0:T(1024)}, f32[768]{0:T(1024)}, f32[768]{0:T(1024)}, /*index=5*/f32[768]{0:T(1024)}, f32[4]{0:T(128)S(1)}) all-reduce(f32[768]{0:T(1024)S(1)} %get-tuple-element.17, f32[768]{0:T(1024)S(1)} %get-tuple-element.25, ...), channel_id=1, replica_groups=mesh['dp'=8,'tensor'=4] {'dp','tensor'}, use_global_device_ids=true, to_apply=%region_16.17 | all-reduce | flops 4612 | bytes 36896 | tf_op jit(solution)/shard_map/psum | solution.py:202
  802.7 4.6 fusion.29
  807.4 183.9 %all-reduce.5.cloned.1.call-done = (f32[768,3,192]{0,2,1:T(8,128)}, f32[192,768]{1,0:T(8,128)}, f32[768,768]{1,0:T(8,128)}, f32[768,768]{1,0:T(8,128)}) async-done(((f32[768,3,192]{0,2,1:T(8,128)}, f32[192,768]{1,0:T(8,128)}, f32[768,768]{1,0:T(8,128)}, f32[768,768]{1,0:T(8,128)}), (f32[768,3,192]{0,2,1:T(8,128)}, f32[192,768]{1,0:T(8,128)}, f32[768,768]{1,0:T(8,128)}, ...) | async-done | bytes 7077904 | tf_op jit(solution)/shard_map/psum | solution.py:214
  991.3 2.9 copy.100
  994.2 2.0 copy.101
  (191 shorter events, 23.6 us)
Async XLA Ops:
  7.2 333.5 %copy-start = (bf16[768,768]{1,0:T(8,128)(2,1)S(1)}, bf16[768,768]{1,0:T(8,128)(2,1)}, u32[]{:S(2)}) copy-start(bf16[768,768]{1,0:T(8,128)(2,1)} %param.27) | copy-start | bytes 3538948
  7.2 7.5 copy-start.55
  7.2 8.9 copy-start.59
  7.2 62.0 %all-gather.4.cloned.1.call-start = ((), (), s32[]{:S(2)}) async-start(), calls=%async_computation.4 | async-start | bytes 9031680 | tf_op jit(solution)/shard_map/all_gather | solution.py:66
  14.7 189.7 %reduce-scatter.5.cloned.1.call-start = ((), (), s32[]{:S(2)}) async-start(), calls=%async_computation.5 | async-start | bytes 9031680 | tf_op jit(solution)/shard_map/reduce_scatter | solution.py:82
  16.8 97.1 %copy-start.31 = (pred[24,196]{1,0:T(8,128)(4,1)}, pred[24,196]{1,0:T(8,128)(4,1)S(1)}, u32[]{:S(2)}) copy-start(pred[24,196]{1,0:T(8,128)(4,1)S(1)} %get-tuple-element.56) | copy-start | bytes 14116
  107.7 5.2 copy-start.2
  113.9 11.1 %copy-start.25 = (f32[24,3,196]{2,1,0:T(4,128)}, f32[24,3,196]{2,1,0:T(4,128)S(1)}, u32[]{:S(2)}) copy-start(f32[24,3,196]{2,1,0:T(4,128)S(1)} %log_add_fusion) | copy-start | bytes 169348
  125.0 7.5 copy-start.29
  139.0 65.4 %copy-start.43 = (f32[768]{0:T(1024)S(1)}, f32[768]{0:T(1024)}, u32[]{:S(2)}) copy-start(f32[768]{0:T(1024)} %param.22) | copy-start | bytes 9220
  139.0 201.6 %all-gather.6.cloned.1.call-start = ((), (), s32[]{:S(2)}) async-start(), calls=%async_computation.7 | async-start | bytes 9031680 | tf_op jit(solution)/shard_map/all_gather | solution.py:119
  140.5 71.1 %copy-start.39 = (f32[1176]{0:T(1024)}, f32[1176]{0:T(1024)S(1)}, u32[]{:S(2)}) copy-start(f32[1176]{0:T(1024)S(1)} %get-tuple-element.46) | copy-start | bytes 14116
  206.7 16.9 %copy-start.35 = (f32[1176]{0:T(1024)}, f32[1176]{0:T(1024)S(1)}, u32[]{:S(2)}) copy-start(f32[1176]{0:T(1024)S(1)} %broadcast_multiply_fusion.4) | copy-start | bytes 14116
  211.6 12.0 %copy-start.46 = (f32[768]{0:T(1024)S(1)}, f32[768]{0:T(1024)}, u32[]{:S(2)}) copy-start(f32[768]{0:T(1024)} %param.23) | copy-start | bytes 9220
  211.6 12.0 %copy-start.52 = (f32[768]{0:T(1024)S(1)}, f32[768]{0:T(1024)}, u32[]{:S(2)}) copy-start(f32[768]{0:T(1024)} %param.24) | copy-start | bytes 9220
  211.6 250.6 %reduce-scatter.7.cloned.1.call-start = ((), (), s32[]{:S(2)}) async-start(), calls=%async_computation.6 | async-start | bytes 9031680 | tf_op jit(solution)/shard_map/reduce_scatter | solution.py:107
  228.7 52.3 %collective-permute-start = (bf16[1176,768]{1,0:T(8,128)(2,1)S(1)}, bf16[1176,768]{1,0:T(8,128)(2,1)S(1)}, u32[]{:S(2)}, u32[]{:S(2)}) collective-permute-start(bf16[1176,768]{1,0:T(8,128)(2,1)S(1)} %get-tuple-element.50), channel_id=1, source_target_pairs={{0,1},{1,2},{2,3},{3,0},{4,5},{5,6},{6,7},{7,4},{8,9},{9,10},{10,1... | collective-permute-start | bytes 5419016 | tf_op jit(solution)/shard_map/ppermute | solution.py:101
  281.1 22.4 %collective-permute-start.1 = (bf16[1176,768]{1,0:T(8,128)(2,1)S(1)}, bf16[1176,768]{1,0:T(8,128)(2,1)}, u32[]{:S(2)}, u32[]{:S(2)}) collective-permute-start(bf16[1176,768]{1,0:T(8,128)(2,1)S(1)} %collective-permute-done), channel_id=1, source_target_pairs={{0,1},{1,2},{2,3},{3,0},{4,5},{5,6},{6,7},{7,4},{8,9},{9,10},{10,1... | collective-permute-start | bytes 5419016 | tf_op jit(solution)/shard_map/ppermute | solution.py:101
  303.5 22.7 %collective-permute-start.2 = (bf16[1176,768]{1,0:T(8,128)(2,1)}, bf16[1176,768]{1,0:T(8,128)(2,1)}, u32[]{:S(2)}, u32[]{:S(2)}) collective-permute-start(bf16[1176,768]{1,0:T(8,128)(2,1)} %collective-permute-done.1), channel_id=1, source_target_pairs={{0,1},{1,2},{2,3},{3,0},{4,5},{5,6},{6,7},{7,4},{8,9},{9,10},{10,1... | collective-permute-start | bytes 5419016 | tf_op jit(solution)/shard_map/ppermute | solution.py:101
  303.5 25.5 %copy-start.56 = (bf16[768,768]{1,0:T(8,128)(2,1)S(1)}, bf16[768,768]{1,0:T(8,128)(2,1)}, u32[]{:S(2)}) copy-start(bf16[768,768]{1,0:T(8,128)(2,1)} %param.25) | copy-start | bytes 3538948
  329.0 11.6 %copy-start.53 = (f32[768]{0:T(1024)S(1)}, f32[768]{0:T(1024)}, u32[]{:S(2)}) copy-start(f32[768]{0:T(1024)} %param.26) | copy-start | bytes 9220
  340.7 41.1 %copy-start.14 = (f32[4704,768]{1,0:T(8,128)S(1)}, f32[4704,768]{1,0:T(8,128)}, u32[]{:S(2)}) copy-start(f32[4704,768]{1,0:T(8,128)} %fusion.74) | copy-start | bytes 43352068
  397.0 133.0 %reduce-scatter.9.cloned.1.call-start = ((), (), s32[]{:S(2)}) async-start(), calls=%async_computation.8 | async-start | bytes 9031680 | tf_op jit(solution)/shard_map/reduce_scatter | solution.py:128
  409.0 120.9 %copy-start.4 = (bf16[1176,768]{1,0:T(8,128)(2,1)S(1)}, bf16[1176,768]{1,0:T(8,128)(2,1)}, u32[]{:S(2)}) copy-start(bf16[1176,768]{1,0:T(8,128)(2,1)} %param.15) | copy-start | bytes 5419012
  409.0 120.9 %copy-start.36 = (f32[1176]{0:T(1024)S(1)}, f32[1176]{0:T(1024)}, u32[]{:S(2)}) copy-start(f32[1176]{0:T(1024)} %copy-done.35) | copy-start | bytes 14116
  409.0 120.9 %copy-start.40 = (f32[1176]{0:T(1024)S(1)}, f32[1176]{0:T(1024)}, u32[]{:S(2)}) copy-start(f32[1176]{0:T(1024)} %copy-done.39) | copy-start | bytes 14116
  409.0 120.9 %copy-start.42 = (f32[1176]{0:T(1024)S(1)}, f32[1176]{0:T(1024)}, u32[]{:S(2)}) copy-start(f32[1176]{0:T(1024)} %copy-done.41) | copy-start | bytes 14116
  409.0 120.9 %copy-start.44 = (f32[768]{0:T(1024)S(1)}, f32[768]{0:T(1024)}, u32[]{:S(2)}) copy-start(f32[768]{0:T(1024)} %param.22) | copy-start | bytes 9220
  409.1 120.9 %copy-start.47 = (f32[768]{0:T(1024)S(1)}, f32[768]{0:T(1024)}, u32[]{:S(2)}) copy-start(f32[768]{0:T(1024)} %param.23) | copy-start | bytes 9220
  409.1 120.9 %copy-start.54 = (f32[768]{0:T(1024)S(1)}, f32[768]{0:T(1024)}, u32[]{:S(2)}) copy-start(f32[768]{0:T(1024)} %param.28) | copy-start | bytes 9220
  409.1 186.6 %all-gather.8.cloned.1.call-start = ((), (), s32[]{:S(2)}) async-start(), calls=%async_computation.9 | async-start | bytes 9031680 | tf_op jit(solution)/shard_map/all_gather | solution.py:140
  530.0 8.3 copy-start.9
  530.0 8.3 copy-start.19
  530.0 8.3 copy-start.20
  540.7 55.0 %copy-start.30 = (bf16[192,768]{1,0:T(8,128)(2,1)S(1)}, bf16[192,768]{1,0:T(8,128)(2,1)}, u32[]{:S(2)}) copy-start(bf16[192,768]{1,0:T(8,128)(2,1)} %param.21) | copy-start | bytes 884740
  543.9 64.8 %copy-start.26 = (f32[24,3,196]{2,1,0:T(4,128)S(1)}, f32[24,3,196]{2,1,0:T(4,128)}, u32[]{:S(2)}) copy-start(f32[24,3,196]{2,1,0:T(4,128)} %copy-done.25) | copy-start | bytes 169348
  543.9 64.8 %copy-start.32 = (pred[24,196]{1,0:T(8,128)(4,1)S(1)}, pred[24,196]{1,0:T(8,128)(4,1)}, u32[]{:S(2)}) copy-start(pred[24,196]{1,0:T(8,128)(4,1)} %copy-done.31) | copy-start | bytes 14116
  543.9 209.2 %reduce-scatter.11.cloned.1.call-start = ((), (), s32[]{:S(2)}) async-start(), calls=%async_computation.10 | async-start | bytes 9031680 | tf_op jit(solution)/shard_map/reduce_scatter | solution.py:183
  602.5 16.2 %slice-start = ((s8[14745600]{0:T(1024)(128)(4,1)}), s8[2162688]{0:T(1024)(128)(4,1)S(1)}, s32[]{:S(2)}) async-start(s8[14745600]{0:T(1024)(128)(4,1)} %bitcast.78), calls=%async_computation.12 | async-start | bytes 4325376
  608.7 10.0 slice-start.1
  608.7 10.0 slice-start.2
  608.7 10.9 %slice-start.3 = ((s8[14745600]{0:T(1024)(128)(4,1)}), s8[4194304]{0:T(1024)(128)(4,1)S(1)}, s32[]{:S(2)}) async-start(s8[14745600]{0:T(1024)(128)(4,1)} %bitcast.78), calls=%async_computation.15 | async-start | bytes 8388608
  608.7 11.5 %copy-start.12 = (bf16[24,196,3,64]{1,0,3,2:T(8,128)(2,1)S(1)}, bf16[24,196,3,64]{1,0,3,2:T(8,128)(2,1)}, u32[]{:S(2)}) copy-start(bf16[24,196,3,64]{1,0,3,2:T(8,128)(2,1)} %reshape.193) | copy-start | bytes 5419012
  608.7 11.5 %copy-start.49 = (f32[3,64]{1,0:T(4,128)S(1)}, f32[3,64]{1,0:T(4,128)}, u32[]{:S(2)}) copy-start(f32[3,64]{1,0:T(4,128)} %add.166) | copy-start | bytes 2308
  631.5 10.2 %copy-start.50 = (f32[3,64]{1,0:T(4,128)S(1)}, f32[3,64]{1,0:T(4,128)}, u32[]{:S(2)}) copy-start(f32[3,64]{1,0:T(4,128)} %add.169) | copy-start | bytes 2308
  641.8 8.8 copy-start.6
  641.8 8.8 copy-start.10
  653.5 7.6 copy-start.13
  674.5 5.3 copy-start.58
  687.7 303.5 %all-reduce.5.cloned.1.call-start = ((), (), s32[]{:S(2)}) async-start(), calls=%async_computation.11 | async-start | bytes 14155776 | tf_op jit(solution)/shard_map/psum | solution.py:214
  687.8 24.0 %slice-start.8 = ((s8[7225344]{0:T(1024)(128)(4,1)}), s8[4194304]{0:T(1024)(128)(4,1)S(1)}, s32[]{:S(2)}) async-start(s8[7225344]{0:T(1024)(128)(4,1)} %bitcast.86), calls=%async_computation.20 | async-start | bytes 8388608
  687.8 26.5 %slice-start.4 = ((s8[5455872]{0:T(1024)(128)(4,1)}), s8[4194304]{0:T(1024)(128)(4,1)S(1)}, s32[]{:S(2)}) async-start(s8[5455872]{0:T(1024)(128)(4,1)} %bitcast.82), calls=%async_computation.16 | async-start | bytes 8388608
  687.8 26.5 %slice-start.6 = ((s8[7225344]{0:T(1024)(128)(4,1)}), s8[4194304]{0:T(1024)(128)(4,1)S(1)}, s32[]{:S(2)}) async-start(s8[7225344]{0:T(1024)(128)(4,1)} %bitcast.84), calls=%async_computation.18 | async-start | bytes 8388608
  699.6 12.2 %copy-start.15 = (bf16[4704,192]{0,1:T(8,128)(2,1)S(1)}, bf16[4704,192]{0,1:T(8,128)(2,1)}, u32[]{:S(2)}) copy-start(bf16[4704,192]{0,1:T(8,128)(2,1)} %convert_element_type.159) | copy-start | bytes 5419012
  699.6 12.2 %slice-start.9 = ((s8[7225344]{0:T(1024)(128)(4,1)}), s8[3031040]{0:T(1024)(128)(4,1)S(1)}, s32[]{:S(2)}) async-start(s8[7225344]{0:T(1024)(128)(4,1)} %bitcast.86), calls=%async_computation.21 | async-start | bytes 6062080
  699.6 14.7 %slice-start.5 = ((s8[5455872]{0:T(1024)(128)(4,1)}), s8[1261568]{0:T(1024)(128)(4,1)S(1)}, s32[]{:S(2)}) async-start(s8[5455872]{0:T(1024)(128)(4,1)} %bitcast.82), calls=%async_computation.17 | async-start | bytes 2523136
  699.6 14.7 %slice-start.7 = ((s8[7225344]{0:T(1024)(128)(4,1)}), s8[3031040]{0:T(1024)(128)(4,1)S(1)}, s32[]{:S(2)}) async-start(s8[7225344]{0:T(1024)(128)(4,1)} %bitcast.84), calls=%async_computation.19 | async-start | bytes 6062080
  720.2 32.8 %copy-start.5 = (bf16[1176,768]{1,0:T(8,128)(2,1)S(1)}, bf16[1176,768]{1,0:T(8,128)(2,1)}, u32[]{:S(2)}) copy-start(bf16[1176,768]{1,0:T(8,128)(2,1)} %param.15) | copy-start | bytes 5419012
  720.2 32.8 %copy-start.34 = (f32[1176]{0:T(1024)S(1)}, f32[1176]{0:T(1024)}, u32[]{:S(2)}) copy-start(f32[1176]{0:T(1024)} %copy-done.33) | copy-start | bytes 14116
  720.2 32.8 %copy-start.38 = (f32[1176]{0:T(1024)S(1)}, f32[1176]{0:T(1024)}, u32[]{:S(2)}) copy-start(f32[1176]{0:T(1024)} %copy-done.37) | copy-start | bytes 14116
  720.2 32.8 %copy-start.48 = (f32[768]{0:T(1024)S(1)}, f32[768]{0:T(1024)}, u32[]{:S(2)}) copy-start(f32[768]{0:T(1024)} %param.17) | copy-start | bytes 9220
  720.3 36.2 %copy-start.51 = (f32[768]{0:T(1024)S(1)}, f32[768]{0:T(1024)}, u32[]{:S(2)}) copy-start(f32[768]{0:T(1024)} %get-tuple-element.26) | copy-start | bytes 9220
  991.3 5.0 copy-start.23
  991.3 6.4 copy-start.22
  (17 other events, 39.0 us)
Sparse Core Ops, SparseCore 0:
  14.8 54.3 all-gather.3
  139.1 65.1 reduce-scatter.4
  211.8 66.7 all-gather.5
  397.1 65.1 reduce-scatter.6
  464.7 65.1 reduce-scatter.8
  544.0 51.6 all-gather.7
  687.9 65.1 reduce-scatter.10
  758.6 232.5 all-reduce.4
